TPU v7x, 32 devices: a whole 2x2x4 slice. The times are simulated.
32 devices in a mesh: freq: 8 (over z, x), tm: 4 (over y, core).
Axes of the slice: x: 2, y: 2, z: 4, core: 2. Of those that a mesh axis runs over, the one named last changes fastest.
Arguments:
- vis: bfloat16 [16, 8, 16, 2, 128, 128], P('freq', 'tm'), may hold values from -6 to 6
- model: bfloat16 [16, 8, 16, 2, 128, 128], P('freq', 'tm'), may hold values from -6 to 6
- block_rows: int32 [16, 8, 16], P('freq', 'tm'), may hold values from 0 to 15
- block_cols: int32 [16, 8, 16], P('freq', 'tm'), may hold values from 0 to 15
- flags: int32 [16, 8, 16], P('freq', 'tm'), may hold values 0 or 1
- prior: float32 [16, 8, 2, 2048], P('freq', 'tm'), may hold values from -6 to 6
- couplings: float32 [3, 2048], replicated, may hold values from 0.1 to 0.6
- damping: float32 [2048], replicated, may hold values from 8 to 128
Outputs:
- gains: float32 [16, 8, 2, 2048], P('freq', 'tm')
- changes: float32 [4], replicated
All inputs are finite; a program needn't handle non-finite values. No bound on the sum of `flags` on one device may be relied on, other than what follows from the above.
Results may differ from a plain program's by a relative error of at most 0.0003.
Values sent between devices are 32-bit elements; how exact they have to be, the bound alone decides.
A program may use at most 64 MiB of HBM per device.

v0:
```python
import functools

import jax
import jax.numpy as jnp
from jax import lax
from jax.experimental import pallas as pl
from jax.experimental.pallas import tpu as pltpu
from jax.sharding import PartitionSpec as P

ITERS = 4
REACH = 2
MESH = pl.DeviceIdType.MESH
F32 = jnp.float32
BF16 = jnp.bfloat16


def split(value):
    high = value.astype(BF16)
    return high, (value - high.astype(F32)).astype(BF16)


def kernel(
    dims,
    vis_ref, model_ref, rows_in, cols_in, flags_in, prior_in, coup_in, damp_in,
    gains_ref, changes_ref,
    rows_ref, cols_ref, flags_ref, prior_ref, coup_ref, damp_ref,
    vbuf, mbuf, wa, wb, gain, prev, coef, from_prior, terms, low, high, early, late,
    stats, all_stats,
    small_sem, load_sem, prior_sem, up_send, down_send, low_recv, high_recv,
    early_send, late_send, early_recv, late_recv, stats_send, stats_recv,
):
    nf, nt, ftiles, ttiles, blks, width, nb = dims
    fi = lax.axis_index("freq")
    ti = lax.axis_index("tm")
    above, below = lax.rem(fi + 1, nf), lax.rem(fi + nf - 1, nf)
    tiles = [(f, t) for f in range(ftiles) for t in range(ttiles)]

    devices = nf * nt
    me = fi * nt + ti

    def peer(step):
        other = lax.rem(me + step, devices)
        return other, {"freq": other // nt, "tm": lax.rem(other, nt)}

    small = [
        pltpu.make_async_copy(src, dst, small_sem.at[n])
        for n, (src, dst) in enumerate((
            (prior_in, prior_ref), (coup_in, coup_ref), (damp_in, damp_ref),
            (rows_in, rows_ref), (cols_in, cols_ref), (flags_in, flags_ref),
        ))
    ]
    for copy in small:
        copy.start()

    def loads(f, t):
        i = f * ttiles + t
        return (
            pltpu.make_async_copy(vis_ref.at[f, t], vbuf.at[i], load_sem.at[0, i]),
            pltpu.make_async_copy(model_ref.at[f, t], mbuf.at[i], load_sem.at[1, i]),
        )

    for f, t in tiles:
        for copy in loads(f, t):
            copy.start()

    barrier = pltpu.get_barrier_semaphore()

    def greet(step, carry):
        pl.semaphore_signal(barrier, inc=1, device_id=peer(step)[1], device_id_type=MESH)
        return carry

    lax.fori_loop(1, devices, greet, 0)
    for copy in small:
        copy.wait()

    for f, t in tiles:
        i = f * ttiles + t
        for c in range(2):
            for n in range(nb):
                gain[i, c, n : n + 1, :] = prior_ref[f, t, c : c + 1, n * width : (n + 1) * width]
    for n in range(nb):
        for c in range(3):
            coef[c, n : n + 1, :] = coup_ref[c : c + 1, n * width : (n + 1) * width]
        coef[3, n : n + 1, :] = damp_ref[0:1, n * width : (n + 1) * width]

    prior_copy = pltpu.make_async_remote_copy(
        src_ref=prior_ref.at[ftiles - 1], dst_ref=from_prior,
        send_sem=prior_sem.at[0], recv_sem=prior_sem.at[1],
        device_id={"freq": above}, device_id_type=MESH,
    )

    def up_copy(k, f, t):
        s = (f - (ftiles - REACH)) * ttiles + t
        return pltpu.make_async_remote_copy(
            src_ref=terms.at[k, f * ttiles + t], dst_ref=low.at[k, s],
            send_sem=up_send.at[k, s], recv_sem=low_recv.at[k, s],
            device_id={"freq": above}, device_id_type=MESH,
        )

    def down_copy(k, f, t):
        s = f * ttiles + t
        return pltpu.make_async_remote_copy(
            src_ref=terms.at[k, f * ttiles + t], dst_ref=high.at[k, s],
            send_sem=down_send.at[k, s], recv_sem=high_recv.at[k, s],
            device_id={"freq": below}, device_id_type=MESH,
        )

    def later_copy(k, f):
        return pltpu.make_async_remote_copy(
            src_ref=terms.at[k, f * ttiles + ttiles - 1], dst_ref=early.at[k, f],
            send_sem=early_send.at[k, f], recv_sem=early_recv.at[k, f],
            device_id={"tm": lax.rem(ti + 1, nt)}, device_id_type=MESH,
        )

    def earlier_copy(k, f):
        return pltpu.make_async_remote_copy(
            src_ref=terms.at[k, f * ttiles], dst_ref=late.at[k, f],
            send_sem=late_send.at[k, f], recv_sem=late_recv.at[k, f],
            device_id={"tm": lax.rem(ti + nt - 1, nt)}, device_id_type=MESH,
        )

    def prepare(i):
        def pair(p, carry):
            for side in range(2):
                b = 2 * p + side
                lo = side * width
                v_re = vbuf[i, b, 0].astype(F32)
                v_im = vbuf[i, b, 1].astype(F32)
                m_re = mbuf[i, b, 0].astype(F32)
                m_im = mbuf[i, b, 1].astype(F32)
                re_hi, re_lo = split(v_re * m_re + v_im * m_im)
                im_hi, im_lo = split(v_re * m_im - v_im * m_re)
                sq_hi, sq_lo = split(m_re * m_re + m_im * m_im)
                wa[i * blks + b, 0:width, 0:width] = re_hi
                wa[i * blks + b, width:, 0:width] = im_hi
                wa[i * blks + b, 0:width, width:] = sq_hi
                wa[i * blks + b, width:, width:] = sq_lo
                wb[i * (blks // 2) + p, 0:width, lo : lo + width] = re_lo
                wb[i * (blks // 2) + p, width:, lo : lo + width] = im_lo
            return carry

        lax.fori_loop(0, blks // 2, pair, 0)

    row_of = lax.broadcasted_iota(jnp.int32, (8, width), 0)
    block_of = lax.broadcasted_iota(jnp.int32, (nb, width), 0)

    def tile_terms(k, f, t):
        i = f * ttiles + t
        total = [jnp.zeros((nb, width), F32) for _ in range(3)]
        for p in range(blks // 2):
            highs, outs, cols = [], [], []
            for b in (2 * p, 2 * p + 1):
                row = rows_ref[f, t, b]
                cols.append(jnp.where(flags_ref[f, t, b] != 0, cols_ref[f, t, b], -1))
                re = jnp.broadcast_to(gain[i, 0, pl.ds(row, 1), :], (8, width))
                im = jnp.broadcast_to(gain[i, 1, pl.ds(row, 1), :], (8, width))
                sq = re * re + im * im
                left = jnp.where(row_of == 0, re, jnp.where(row_of == 1, im, sq))
                right = jnp.where(row_of == 0, -im, jnp.where(row_of == 1, re, sq))
                lhs = jnp.concatenate([left, right], axis=1)
                lhs_hi = lhs.astype(BF16).astype(F32)
                highs.append(lhs_hi)
                lhs = jnp.concatenate([lhs_hi, lhs - lhs_hi], axis=0).astype(BF16)
                out = jnp.dot(lhs, wa[i * blks + b], preferred_element_type=F32)
                outs.append(out[0:8] + out[8:16])
            low_out = jnp.dot(
                jnp.concatenate(highs, axis=0).astype(BF16),
                wb[i * (blks // 2) + p],
                preferred_element_type=F32,
            )
            low_outs = (low_out[0:8, 0:width], low_out[8:16, width:])
            for out, low_out, col in zip(outs, low_outs, cols):
                num = out[:, 0:width] + low_out
                den = out[:, width:]
                hit = block_of == col
                parts = (num[0:1], num[1:2], den[2:3])
                total = [
                    acc + jnp.where(hit, jnp.broadcast_to(one, (nb, width)), 0.0)
                    for acc, one in zip(total, parts)
                ]
        for c in range(3):
            terms[k, i, c] = total[c]

    def iteration(k, first):
        for f, t in tiles:
            i = f * ttiles + t
            if first:
                for copy in loads(f, t):
                    copy.wait()
                prepare(i)
            tile_terms(k, f, t)
            if first and i == 0:
                pl.semaphore_wait(barrier, devices - 1)
                prior_copy.start()
            if f >= ftiles - REACH:
                up_copy(k, f, t).start()
            if f < REACH:
                down_copy(k, f, t).start()
            if t == ttiles - 1:
                later_copy(k, f).start()
            if t == 0:
                earlier_copy(k, f).start()

        if first:
            prior_copy.wait_recv()
            for f, t in tiles:
                i = f * ttiles + t
                for c in range(2):
                    if f == 0:
                        for n in range(nb):
                            prev[i, c, n : n + 1, :] = from_prior[
                                t, c : c + 1, n * width : (n + 1) * width
                            ]
                        prev[i, c] = prev[i, c] * coef[3]
                    else:
                        prev[i, c] = gain[i - ttiles, c] * coef[3]

        for f in range(ftiles):
            later_copy(k, f).wait_recv()
            earlier_copy(k, f).wait_recv()
        for f in range(ftiles - REACH, ftiles):
            for t in range(ttiles):
                up_copy(k, f, t).wait_recv()
        for f in range(REACH):
            for t in range(ttiles):
                down_copy(k, f, t).wait_recv()

        def at(f, t, c):
            if t < 0:
                return jnp.where(ti > 0, early[k, f, c], 0.0)
            if t >= ttiles:
                return jnp.where(ti < nt - 1, late[k, f, c], 0.0)
            if f < 0:
                return low[k, (f + REACH) * ttiles + t, c]
            if f >= ftiles:
                return high[k, (f - ftiles) * ttiles + t, c]
            return terms[k, f * ttiles + t, c]

        odd = lax.rem(k, 2) == 1
        change = jnp.zeros((nb, width), F32)
        scale = jnp.zeros((nb, width), F32)
        for f, t in tiles:
            i = f * ttiles + t
            sums = [
                at(f, t, c)
                + coef[0] * (at(f - 1, t, c) + at(f + 1, t, c))
                + coef[1] * (at(f - 2, t, c) + at(f + 2, t, c))
                + coef[2] * (at(f, t - 1, c) + at(f, t + 1, c))
                for c in range(3)
            ]
            denom = sums[2] + coef[3]
            for c in range(2):
                old = gain[i, c]
                fresh = (sums[c] + prev[i, c]) / denom
                fresh = jnp.where(odd, 0.5 * (fresh + old), fresh)
                diff = fresh - old
                change = change + diff * diff
                scale = scale + fresh * fresh
                gain[i, c] = fresh
        sums = [
            jnp.sum(jnp.sum(x, axis=0, keepdims=True), axis=1, keepdims=True)
            for x in (change, scale)
        ]
        stats[...] = jnp.where(lane_of == k, jnp.concatenate(sums, axis=0), stats[...])

    lane_of = lax.broadcasted_iota(jnp.int32, (2, width), 1)
    stats[...] = jnp.zeros_like(stats)
    iteration(0, True)

    def rest(k, carry):
        iteration(k, False)
        return carry

    lax.fori_loop(1, ITERS, rest, 0)

    def stats_copy(step, slot):
        return pltpu.make_async_remote_copy(
            src_ref=stats, dst_ref=all_stats.at[slot],
            send_sem=stats_send.at[step], recv_sem=stats_recv.at[slot],
            device_id=peer(step)[1], device_id_type=MESH,
        )

    def send_stats(step, carry):
        stats_copy(step, me).start()
        return carry

    lax.fori_loop(1, devices, send_stats, 0)
    all_stats[me] = stats[...]

    for f, t in tiles:
        i = f * ttiles + t
        for c in range(2):
            for n in range(nb):
                gains_ref[f, t, c : c + 1, n * width : (n + 1) * width] = gain[i, c, n : n + 1, :]

    def drain(k, carry):
        for f, t in tiles:
            if f >= ftiles - REACH:
                up_copy(k, f, t).wait_send()
            if f < REACH:
                down_copy(k, f, t).wait_send()
        for f in range(ftiles):
            later_copy(k, f).wait_send()
            earlier_copy(k, f).wait_send()
        return carry

    lax.fori_loop(0, ITERS, drain, 0)
    prior_copy.wait_send()

    def finish(step, carry):
        stats_copy(step, me).wait_send()
        stats_copy(step, peer(step)[0]).wait_recv()
        return carry

    lax.fori_loop(1, devices, finish, 0)
    whole = jnp.sum(all_stats[...], axis=0)
    changes_ref[...] = jnp.sqrt(whole[0:1] / (whole[1:2] + 1e-06))


def per_device(vis, model, block_rows, block_cols, flags, prior, couplings, damping):
    nf, nt = lax.axis_size("freq"), lax.axis_size("tm")
    ftiles, ttiles, blks = vis.shape[:3]
    width = vis.shape[-1]
    nb = prior.shape[-1] // width
    count = ftiles * ttiles
    dims = (nf, nt, ftiles, ttiles, blks, width, nb)
    vmem = pl.BlockSpec(memory_space=pltpu.VMEM)
    hbm = pl.BlockSpec(memory_space=pltpu.HBM)
    dma = pltpu.SemaphoreType.DMA
    halo = REACH * ttiles
    gains, changes = pl.pallas_call(
        functools.partial(kernel, dims),
        name="stefcal",
        out_shape=(
            jax.ShapeDtypeStruct(prior.shape, F32),
            jax.ShapeDtypeStruct((1, width), F32),
        ),
        in_specs=[hbm] * 8,
        out_specs=(vmem, vmem),
        scratch_shapes=[
            pltpu.SMEM(block_rows.shape, jnp.int32),
            pltpu.SMEM(block_rows.shape, jnp.int32),
            pltpu.SMEM(block_rows.shape, jnp.int32),
            pltpu.VMEM(prior.shape, F32),
            pltpu.VMEM(couplings.shape, F32),
            pltpu.VMEM((1, damping.shape[0]), F32),
            pltpu.VMEM((count,) + vis.shape[2:], BF16),
            pltpu.VMEM((count,) + vis.shape[2:], BF16),
            pltpu.VMEM((count * blks, 2 * width, 2 * width), BF16),
            pltpu.VMEM((count * blks // 2, 2 * width, 2 * width), BF16),
            pltpu.VMEM((count, 2, nb, width), F32),
            pltpu.VMEM((count, 2, nb, width), F32),
            pltpu.VMEM((4, nb, width), F32),
            pltpu.VMEM(prior.shape[1:], F32),
            pltpu.VMEM((ITERS, count, 3, nb, width), F32),
            pltpu.VMEM((ITERS, halo, 3, nb, width), F32),
            pltpu.VMEM((ITERS, halo, 3, nb, width), F32),
            pltpu.VMEM((ITERS, ftiles, 3, nb, width), F32),
            pltpu.VMEM((ITERS, ftiles, 3, nb, width), F32),
            pltpu.VMEM((2, width), F32),
            pltpu.VMEM((nf * nt, 2, width), F32),
            dma((6,)),
            dma((2, count)),
            dma((2,)),
            dma((ITERS, halo)),
            dma((ITERS, halo)),
            dma((ITERS, halo)),
            dma((ITERS, halo)),
            dma((ITERS, ftiles)),
            dma((ITERS, ftiles)),
            dma((ITERS, ftiles)),
            dma((ITERS, ftiles)),
            dma((nf * nt,)),
            dma((nf * nt,)),
        ],
        compiler_params=pltpu.CompilerParams(
            collective_id=0, has_side_effects=True, vmem_limit_bytes=67043328
        ),
    )(vis, model, block_rows, block_cols, flags, prior, couplings, damping.reshape(1, -1))
    return gains, changes[0, :ITERS]


def solution(mesh):
    placed = (
        P("freq", "tm", None, None, None, None),
        P("freq", "tm", None, None, None, None),
        P("freq", "tm", None),
        P("freq", "tm", None),
        P("freq", "tm", None),
        P("freq", "tm", None, None),
        P(),
        P(),
    )
    return jax.shard_map(
        per_device,
        mesh=mesh,
        in_specs=placed,
        out_specs=(P("freq", "tm", None, None), P()),
        check_vma=False,
    )
```

profile of v0, /device:TPU:0, one launch (start us, length us, event | category | flops | bytes accessed | tf_op | source)
XLA Modules:
  0.0 46.1 jit_solution(10804100489541264634)
XLA Ops:
  0.6 42.9 %stefcal.1 = (f32[2,2,2,2048]{3,2,1,0:T(2,128)}, f32[1,128]{1,0:T(1,128)}) custom-call(bf16[2,2,16,2,128,128]{5,4,3,2,1,0:T(8,128)(2,1)} %vis_ref.1, bf16[2,2,16,2,128,128]{5,4,3,2,1,0:T(8,128)(2,1)} %model_ref.1, s32[2,2,16]{2,1,0:T(2,128)} %rows_in.1, s32[2,2,16]{2,1,0:T(2,128)} %cols_in.1, s32[2,2,16]{2,1,0:T(2,128)} %flags_in.1, ...), custom_call_target="tpu_custom_call" | custom-call | tf_op jit(solution)/shard_map/stefcal/pallas_call | solution.py:331
  43.5 1.1 %slice_bitcast_fusion = f32[4]{0:T(128)} fusion(f32[1,128]{1,0:T(1,128)} %get-tuple-element.5), kind=kLoop, calls=%fused_computation | loop fusion | bytes 32 | tf_op jit(solution)/shard_map/squeeze | solution.py:380
  44.7 1.5 %copy.11 = f32[2,2,2,2048]{3,2,1,0:T(2,128)} copy(f32[2,2,2,2048]{3,2,1,0:T(2,128)} %get-tuple-element.8) | data formatting | bytes 131072
where the time goes:
time: 46.3 us; the launch traced here: 46.1 us
  Pallas kernels  42.9 us (93%)
  local copies, waits for them, and re-layouts  2.59 us (6%)
  between operations  0.64 us (1%)
    pallas_call x1, Pallas kernels, per_device(): pl.pallas_call(functools.partial(kernel, dims), name='stefcal', out_shape...  42.9 us
    unnamed x1, local copies, waits for them, and re-layouts  1.47 us
    squeeze x1, local copies, waits for them, and re-layouts, per_device(): return (gains, changes[0, :ITERS])  1.12 us

commit v1 on v0

--- a/solution.py
+++ b/solution.py
@@ -33,7 +33,10 @@
     fi = lax.axis_index("freq")
     ti = lax.axis_index("tm")
     above, below = lax.rem(fi + 1, nf), lax.rem(fi + nf - 1, nf)
-    tiles = [(f, t) for f in range(ftiles) for t in range(ttiles)]
+    tiles = [(f, t) for t in range(ttiles) for f in range(ftiles)]
+
+    def at_tile(f, t):
+        return t * ftiles + f
 
     devices = nf * nt
     me = fi * nt + ti
@@ -53,7 +56,7 @@
         copy.start()
 
     def loads(f, t):
-        i = f * ttiles + t
+        i = at_tile(f, t)
         return (
             pltpu.make_async_copy(vis_ref.at[f, t], vbuf.at[i], load_sem.at[0, i]),
             pltpu.make_async_copy(model_ref.at[f, t], mbuf.at[i], load_sem.at[1, i]),
@@ -74,7 +77,7 @@
         copy.wait()
 
     for f, t in tiles:
-        i = f * ttiles + t
+        i = at_tile(f, t)
         for c in range(2):
             for n in range(nb):
                 gain[i, c, n : n + 1, :] = prior_ref[f, t, c : c + 1, n * width : (n + 1) * width]
@@ -90,31 +93,31 @@
     )
 
     def up_copy(k, f, t):
-        s = (f - (ftiles - REACH)) * ttiles + t
+        s = t * REACH + f - (ftiles - REACH)
         return pltpu.make_async_remote_copy(
-            src_ref=terms.at[k, f * ttiles + t], dst_ref=low.at[k, s],
+            src_ref=terms.at[k, at_tile(f, t)], dst_ref=low.at[k, s],
             send_sem=up_send.at[k, s], recv_sem=low_recv.at[k, s],
             device_id={"freq": above}, device_id_type=MESH,
         )
 
     def down_copy(k, f, t):
-        s = f * ttiles + t
+        s = t * REACH + f
         return pltpu.make_async_remote_copy(
-            src_ref=terms.at[k, f * ttiles + t], dst_ref=high.at[k, s],
+            src_ref=terms.at[k, at_tile(f, t)], dst_ref=high.at[k, s],
             send_sem=down_send.at[k, s], recv_sem=high_recv.at[k, s],
             device_id={"freq": below}, device_id_type=MESH,
         )
 
     def later_copy(k, f):
         return pltpu.make_async_remote_copy(
-            src_ref=terms.at[k, f * ttiles + ttiles - 1], dst_ref=early.at[k, f],
+            src_ref=terms.at[k, at_tile(f, ttiles - 1)], dst_ref=early.at[k, f],
             send_sem=early_send.at[k, f], recv_sem=early_recv.at[k, f],
             device_id={"tm": lax.rem(ti + 1, nt)}, device_id_type=MESH,
         )
 
     def earlier_copy(k, f):
         return pltpu.make_async_remote_copy(
-            src_ref=terms.at[k, f * ttiles], dst_ref=late.at[k, f],
+            src_ref=terms.at[k, at_tile(f, 0)], dst_ref=late.at[k, f],
             send_sem=late_send.at[k, f], recv_sem=late_recv.at[k, f],
             device_id={"tm": lax.rem(ti + nt - 1, nt)}, device_id_type=MESH,
         )
@@ -145,7 +148,7 @@
     block_of = lax.broadcasted_iota(jnp.int32, (nb, width), 0)
 
     def tile_terms(k, f, t):
-        i = f * ttiles + t
+        i = at_tile(f, t)
         total = [jnp.zeros((nb, width), F32) for _ in range(3)]
         for p in range(blks // 2):
             highs, outs, cols = [], [], []
@@ -181,66 +184,42 @@
         for c in range(3):
             terms[k, i, c] = total[c]
 
-    def iteration(k, first):
-        for f, t in tiles:
-            i = f * ttiles + t
-            if first:
-                for copy in loads(f, t):
-                    copy.wait()
-                prepare(i)
-            tile_terms(k, f, t)
-            if first and i == 0:
-                pl.semaphore_wait(barrier, devices - 1)
-                prior_copy.start()
-            if f >= ftiles - REACH:
-                up_copy(k, f, t).start()
-            if f < REACH:
-                down_copy(k, f, t).start()
+    def send(k, f, t):
+        if t == ttiles - 1:
+            later_copy(k, f).start()
+        if t == 0:
+            earlier_copy(k, f).start()
+        if f >= ftiles - REACH:
+            up_copy(k, f, t).start()
+        if f < REACH:
+            down_copy(k, f, t).start()
+
+    def arrived(k, t):
+        for f in range(ftiles):
+            if t == 0:
+                later_copy(k, f).wait_recv()
             if t == ttiles - 1:
-                later_copy(k, f).start()
-            if t == 0:
-                earlier_copy(k, f).start()
-
-        if first:
-            prior_copy.wait_recv()
-            for f, t in tiles:
-                i = f * ttiles + t
-                for c in range(2):
-                    if f == 0:
-                        for n in range(nb):
-                            prev[i, c, n : n + 1, :] = from_prior[
-                                t, c : c + 1, n * width : (n + 1) * width
-                            ]
-                        prev[i, c] = prev[i, c] * coef[3]
-                    else:
-                        prev[i, c] = gain[i - ttiles, c] * coef[3]
-
-        for f in range(ftiles):
-            later_copy(k, f).wait_recv()
-            earlier_copy(k, f).wait_recv()
+                earlier_copy(k, f).wait_recv()
         for f in range(ftiles - REACH, ftiles):
-            for t in range(ttiles):
-                up_copy(k, f, t).wait_recv()
+            up_copy(k, f, t).wait_recv()
         for f in range(REACH):
-            for t in range(ttiles):
-                down_copy(k, f, t).wait_recv()
-
+            down_copy(k, f, t).wait_recv()
+
+    def update(k, t, change, scale):
         def at(f, t, c):
             if t < 0:
                 return jnp.where(ti > 0, early[k, f, c], 0.0)
             if t >= ttiles:
                 return jnp.where(ti < nt - 1, late[k, f, c], 0.0)
             if f < 0:
-                return low[k, (f + REACH) * ttiles + t, c]
+                return low[k, t * REACH + f + REACH, c]
             if f >= ftiles:
-                return high[k, (f - ftiles) * ttiles + t, c]
-            return terms[k, f * ttiles + t, c]
+                return high[k, t * REACH + f - ftiles, c]
+            return terms[k, at_tile(f, t), c]
 
         odd = lax.rem(k, 2) == 1
-        change = jnp.zeros((nb, width), F32)
-        scale = jnp.zeros((nb, width), F32)
-        for f, t in tiles:
-            i = f * ttiles + t
+        for f in range(ftiles):
+            i = at_tile(f, t)
             sums = [
                 at(f, t, c)
                 + coef[0] * (at(f - 1, t, c) + at(f + 1, t, c))
@@ -257,26 +236,64 @@
                 change = change + diff * diff
                 scale = scale + fresh * fresh
                 gain[i, c] = fresh
-        sums = [
-            jnp.sum(jnp.sum(x, axis=0, keepdims=True), axis=1, keepdims=True)
-            for x in (change, scale)
-        ]
-        stats[...] = jnp.where(lane_of == k, jnp.concatenate(sums, axis=0), stats[...])
-
-    lane_of = lax.broadcasted_iota(jnp.int32, (2, width), 1)
+        return change, scale
+
+    def record(k, change, scale):
+        row = stats[...]
+        for lane, value in ((k, change), (ITERS + k, scale)):
+            total = jnp.sum(jnp.sum(value, axis=0, keepdims=True), axis=1, keepdims=True)
+            row = jnp.where(lane_of == lane, total, row)
+        stats[...] = row
+
+    lane_of = lax.broadcasted_iota(jnp.int32, (1, width), 1)
     stats[...] = jnp.zeros_like(stats)
-    iteration(0, True)
-
-    def rest(k, carry):
-        iteration(k, False)
+    zero = jnp.zeros((nb, width), F32)
+
+    for f, t in tiles:
+        for copy in loads(f, t):
+            copy.wait()
+        prepare(at_tile(f, t))
+        tile_terms(0, f, t)
+        if at_tile(f, t) == 0:
+            pl.semaphore_wait(barrier, devices - 1)
+            prior_copy.start()
+        send(0, f, t)
+
+    prior_copy.wait_recv()
+    for f, t in tiles:
+        i = at_tile(f, t)
+        for c in range(2):
+            if f == 0:
+                for n in range(nb):
+                    prev[i, c, n : n + 1, :] = from_prior[
+                        t, c : c + 1, n * width : (n + 1) * width
+                    ]
+                prev[i, c] = prev[i, c] * coef[3]
+            else:
+                prev[i, c] = gain[at_tile(f - 1, t), c] * coef[3]
+
+    def step(k, carry):
+        change, scale = zero, zero
+        for t in range(ttiles):
+            arrived(k, t)
+            change, scale = update(k, t, change, scale)
+            for f in range(ftiles):
+                tile_terms(k + 1, f, t)
+                send(k + 1, f, t)
+        record(k, change, scale)
         return carry
 
-    lax.fori_loop(1, ITERS, rest, 0)
-
-    def stats_copy(step, slot):
+    lax.fori_loop(0, ITERS - 1, step, 0)
+    change, scale = zero, zero
+    for t in range(ttiles):
+        arrived(ITERS - 1, t)
+        change, scale = update(ITERS - 1, t, change, scale)
+    record(ITERS - 1, change, scale)
+
+    def stats_copy(step, row):
         return pltpu.make_async_remote_copy(
-            src_ref=stats, dst_ref=all_stats.at[slot],
-            send_sem=stats_send.at[step], recv_sem=stats_recv.at[slot],
+            src_ref=stats, dst_ref=all_stats.at[pl.ds(row, 1)],
+            send_sem=stats_send.at[step], recv_sem=stats_recv.at[row],
             device_id=peer(step)[1], device_id_type=MESH,
         )
 
@@ -285,10 +302,10 @@
         return carry
 
     lax.fori_loop(1, devices, send_stats, 0)
-    all_stats[me] = stats[...]
+    all_stats[pl.ds(me, 1), :] = stats[...]
 
     for f, t in tiles:
-        i = f * ttiles + t
+        i = at_tile(f, t)
         for c in range(2):
             for n in range(nb):
                 gains_ref[f, t, c : c + 1, n * width : (n + 1) * width] = gain[i, c, n : n + 1, :]
@@ -313,8 +330,15 @@
         return carry
 
     lax.fori_loop(1, devices, finish, 0)
-    whole = jnp.sum(all_stats[...], axis=0)
-    changes_ref[...] = jnp.sqrt(whole[0:1] / (whole[1:2] + 1e-06))
+    whole = jnp.sum(all_stats[...], axis=0, keepdims=True)
+    below_it = pltpu.roll(whole, width - ITERS, axis=1)
+    changes_ref[...] = jnp.sqrt(whole / (below_it + 1e-06))
+
+
+def hand_on(gains_in, changes_in, gains_ref, changes_ref):
+    gains_ref[...] = gains_in[...]
+    for k in range(ITERS):
+        changes_ref[k] = changes_in[0, k]
 
 
 def per_device(vis, model, block_rows, block_cols, flags, prior, couplings, damping):
@@ -357,8 +381,8 @@
             pltpu.VMEM((ITERS, halo, 3, nb, width), F32),
             pltpu.VMEM((ITERS, ftiles, 3, nb, width), F32),
             pltpu.VMEM((ITERS, ftiles, 3, nb, width), F32),
-            pltpu.VMEM((2, width), F32),
-            pltpu.VMEM((nf * nt, 2, width), F32),
+            pltpu.VMEM((1, width), F32),
+            pltpu.VMEM((nf * nt, width), F32),
             dma((6,)),
             dma((2, count)),
             dma((2,)),
@@ -377,7 +401,17 @@
             collective_id=0, has_side_effects=True, vmem_limit_bytes=67043328
         ),
     )(vis, model, block_rows, block_cols, flags, prior, couplings, damping.reshape(1, -1))
-    return gains, changes[0, :ITERS]
+    smem = pl.BlockSpec(memory_space=pltpu.SMEM)
+    return pl.pallas_call(
+        hand_on,
+        name="hand_on",
+        out_shape=(
+            jax.ShapeDtypeStruct(prior.shape, F32),
+            jax.ShapeDtypeStruct((ITERS,), F32),
+        ),
+        in_specs=[vmem, smem],
+        out_specs=(vmem, smem),
+    )(gains, changes)
 
 
 def solution(mesh):

time: 46.3 us -> 41.2 us (0.89)
  local copies, waits for them, and re-layouts: 2.59 us -> 0 us
  Pallas kernels: 42.9 us -> 40.4 us
    pallas_call x1, Pallas kernels: 42.9 us -> 38.9 us  [per_device(): pl.pallas_call(functools.partial(kernel, dims), name='stefcal', out_shape...]
    pallas_call x0 -> x1, Pallas kernels: none -> 1.49 us  [per_device(): pl.pallas_call(hand_on, name='hand_on', out_shape=(jax.ShapeDtypeStruct(p...]
    unnamed x1 -> x0, local copies, waits for them, and re-layouts: 1.47 us -> none
    squeeze x1 -> x0, local copies, waits for them, and re-layouts: 1.12 us -> none  [per_device(): return (gains, changes[0, :ITERS])]
where the time goes in v1:
time: 41.2 us; the launch traced here: 41 us
  Pallas kernels  40.4 us (98%)
  between operations  0.64 us (2%)
    pallas_call x1, Pallas kernels, per_device(): pl.pallas_call(functools.partial(kernel, dims), name='stefcal', out_shape...  38.9 us
    pallas_call x1, Pallas kernels, per_device(): pl.pallas_call(hand_on, name='hand_on', out_shape=(jax.ShapeDtypeStruct(p...  1.49 us

profile of v1, /device:TPU:0, one launch (start us, length us, event | category | flops | bytes accessed | tf_op | source)
XLA Modules:
  0.0 41.0 jit_solution(881216775179864447)
XLA Ops:
  0.6 38.9 %stefcal.1 = (f32[2,2,2,2048]{3,2,1,0:T(2,128)}, f32[1,128]{1,0:T(1,128)}) custom-call(bf16[2,2,16,2,128,128]{5,4,3,2,1,0:T(8,128)(2,1)} %vis_ref.1, bf16[2,2,16,2,128,128]{5,4,3,2,1,0:T(8,128)(2,1)} %model_ref.1, s32[2,2,16]{2,1,0:T(2,128)} %rows_in.1, s32[2,2,16]{2,1,0:T(2,128)} %cols_in.1, s32[2,2,16]{2,1,0:T(2,128)} %flags_in.1, ...), custom_call_target="tpu_custom_call" | custom-call | tf_op jit(solution)/shard_map/stefcal/pallas_call | solution.py:355
  39.5 1.5 %hand_on.1 = (f32[2,2,2,2048]{3,2,1,0:T(2,128)}, f32[4]{0:T(128)}) custom-call(f32[2,2,2,2048]{3,2,1,0:T(2,128)} %get-tuple-element.4.gains_in, f32[1,128]{1,0:T(1,128)} %get-tuple-element.5.changes_in), custom_call_target="tpu_custom_call" | custom-call | tf_op jit(solution)/shard_map/hand_on/pallas_call | solution.py:405

commit v2 on v1

v2 whole, which is shorter than its diff:
```python
import functools

import jax
import jax.numpy as jnp
from jax import lax
from jax.experimental import pallas as pl
from jax.experimental.pallas import tpu as pltpu
from jax.sharding import PartitionSpec as P

ITERS = 4
REACH = 2
MEET = 0
UNROLL = 8
MESH = pl.DeviceIdType.MESH
LOGICAL = pl.DeviceIdType.LOGICAL
F32 = jnp.float32
BF16 = jnp.bfloat16


def split(value):
    high = value.astype(BF16)
    return high, (value - high.astype(F32)).astype(BF16)


def kernel(
    dims,
    vis_ref, model_ref, rows_in, cols_in, flags_in, prior_in, coup_in, damp_in,
    gains_ref, all_stats_ref,
    rows_ref, cols_ref, flags_ref, prior_ref, coup_ref, damp_ref,
    data, wa, wb, gain, prev, coef, from_prior, terms, halo, early, late,
    stats,
    small_sem, load_sem, prior_sem, halo_send, halo_recv,
    early_send, late_send, early_recv, late_recv, stats_send, stats_recv, out_sem,
):
    nf, nt, ftiles, ttiles, blks, width, nb = dims
    fi = lax.axis_index("freq")
    ti = lax.axis_index("tm")
    above, below = lax.rem(fi + 1, nf), lax.rem(fi + nf - 1, nf)
    tiles = [(f, t) for t in range(ttiles) for f in range(ftiles)]

    def at_tile(f, t):
        return t * ftiles + f

    devices = nf * nt
    me = fi * nt + ti

    def peer(step):
        return lax.rem(me + step, devices)

    def loads(f, t):
        i = at_tile(f, t)
        return (
            pltpu.make_async_copy(vis_ref.at[f, t], data.at[i, 0], load_sem.at[i]),
            pltpu.make_async_copy(model_ref.at[f, t], data.at[i, 1], load_sem.at[i]),
        )

    for copy in loads(*tiles[0]):
        copy.start()
    small = [
        pltpu.make_async_copy(src, dst, small_sem.at[n])
        for n, (src, dst) in enumerate((
            (prior_in, prior_ref), (coup_in, coup_ref), (damp_in, damp_ref),
            (rows_in, rows_ref), (cols_in, cols_ref), (flags_in, flags_ref),
        ))
    ]
    for copy in small:
        copy.start()
    for f, t in tiles[1:]:
        for copy in loads(f, t):
            copy.start()

    barrier = pltpu.get_barrier_semaphore()

    def greet(step, carry):
        pl.semaphore_signal(barrier, inc=1, device_id=peer(step), device_id_type=LOGICAL)
        return carry

    lax.fori_loop(1, devices, greet, 0, unroll=UNROLL)

    def set_up():
        for f, t in tiles:
            i = at_tile(f, t)
            for c in range(2):
                for n in range(nb):
                    gain[i, c, n : n + 1, :] = prior_ref[f, t, c : c + 1, n * width : (n + 1) * width]
        for n in range(nb):
            for c in range(3):
                coef[c, n : n + 1, :] = coup_ref[c : c + 1, n * width : (n + 1) * width]
            coef[3, n : n + 1, :] = damp_ref[0:1, n * width : (n + 1) * width]

    prior_copy = pltpu.make_async_remote_copy(
        src_ref=prior_ref.at[ftiles - 1], dst_ref=from_prior,
        send_sem=prior_sem.at[0], recv_sem=prior_sem.at[1],
        device_id={"freq": above}, device_id_type=MESH,
    )

    def up_copy(k, f, t):
        return pltpu.make_async_remote_copy(
            src_ref=terms.at[k, at_tile(f, t)], dst_ref=halo.at[k, t, f - (ftiles - REACH)],
            send_sem=halo_send.at[0], recv_sem=halo_recv.at[k, t],
            device_id={"freq": above}, device_id_type=MESH,
        )

    def down_copy(k, f, t):
        return pltpu.make_async_remote_copy(
            src_ref=terms.at[k, at_tile(f, t)], dst_ref=halo.at[k, t, REACH + f],
            send_sem=halo_send.at[0], recv_sem=halo_recv.at[k, t],
            device_id={"freq": below}, device_id_type=MESH,
        )

    def later_copy(k, f):
        return pltpu.make_async_remote_copy(
            src_ref=terms.at[k, at_tile(f, ttiles - 1)], dst_ref=early.at[k, f],
            send_sem=early_send.at[0], recv_sem=early_recv.at[k],
            device_id={"tm": lax.rem(ti + 1, nt)}, device_id_type=MESH,
        )

    def earlier_copy(k, f):
        return pltpu.make_async_remote_copy(
            src_ref=terms.at[k, at_tile(f, 0)], dst_ref=late.at[k, f],
            send_sem=late_send.at[0], recv_sem=late_recv.at[k],
            device_id={"tm": lax.rem(ti + nt - 1, nt)}, device_id_type=MESH,
        )

    def wait_for(ref, sem):
        pltpu.make_async_copy(ref, ref, sem).wait()

    def prepare(i, p):
        for side in range(2):
            b = 2 * p + side
            lo = side * width
            v_re = data[i, 0, b, 0].astype(F32)
            v_im = data[i, 0, b, 1].astype(F32)
            m_re = data[i, 1, b, 0].astype(F32)
            m_im = data[i, 1, b, 1].astype(F32)
            re_hi, re_lo = split(v_re * m_re + v_im * m_im)
            im_hi, im_lo = split(v_re * m_im - v_im * m_re)
            sq_hi, sq_lo = split(m_re * m_re + m_im * m_im)
            wa[i * blks + b, 0:width, 0:width] = re_hi
            wa[i * blks + b, width:, 0:width] = im_hi
            wa[i * blks + b, 0:width, width:] = sq_hi
            wa[i * blks + b, width:, width:] = sq_lo
            wb[i * (blks // 2) + p, 0:width, lo : lo + width] = re_lo
            wb[i * (blks // 2) + p, width:, lo : lo + width] = im_lo

    row_of = lax.broadcasted_iota(jnp.int32, (8, width), 0)
    block_of = lax.broadcasted_iota(jnp.int32, (nb, width), 0)
    zero = jnp.zeros((nb, width), F32)

    def pair_terms(f, t, p, total):
        i = at_tile(f, t)
        highs, outs, cols = [], [], []
        for b in (2 * p, 2 * p + 1):
            row = rows_ref[f, t, b]
            cols.append(jnp.where(flags_ref[f, t, b] != 0, cols_ref[f, t, b], -1))
            re = jnp.broadcast_to(gain[i, 0, pl.ds(row, 1), :], (8, width))
            im = jnp.broadcast_to(gain[i, 1, pl.ds(row, 1), :], (8, width))
            sq = re * re + im * im
            left = jnp.where(row_of == 0, re, jnp.where(row_of == 1, im, sq))
            right = jnp.where(row_of == 0, -im, jnp.where(row_of == 1, re, sq))
            lhs = jnp.concatenate([left, right], axis=1)
            lhs_hi = lhs.astype(BF16).astype(F32)
            highs.append(lhs_hi)
            lhs = jnp.concatenate([lhs_hi, lhs - lhs_hi], axis=0).astype(BF16)
            out = jnp.dot(lhs, wa[i * blks + b], preferred_element_type=F32)
            outs.append(out[0:8] + out[8:16])
        low_out = jnp.dot(
            jnp.concatenate(highs, axis=0).astype(BF16),
            wb[i * (blks // 2) + p],
            preferred_element_type=F32,
        )
        low_outs = (low_out[0:8, 0:width], low_out[8:16, width:])
        for out, low_out, col in zip(outs, low_outs, cols):
            num = out[:, 0:width] + low_out
            den = out[:, width:]
            hit = block_of == col
            parts = (num[0:1], num[1:2], den[2:3])
            total = [
                acc + jnp.where(hit, jnp.broadcast_to(one, (nb, width)), 0.0)
                for acc, one in zip(total, parts)
            ]
        return total

    def keep(k, f, t, total):
        for c in range(3):
            terms[k, at_tile(f, t), c] = total[c]

    def tile_terms(k, f, t):
        total = [zero] * 3
        for p in range(blks // 2):
            total = pair_terms(f, t, p, total)
        keep(k, f, t, total)

    def send(k, f, t):
        if t == ttiles - 1:
            pl.when(ti < nt - 1)(later_copy(k, f).start)
        if t == 0:
            pl.when(ti > 0)(earlier_copy(k, f).start)
        if f >= ftiles - REACH:
            up_copy(k, f, t).start()
        if f < REACH:
            down_copy(k, f, t).start()

    def arrived(k, t):
        if t == 0:
            pl.when(ti > 0)(lambda: wait_for(early.at[k], early_recv.at[k]))
        if t == ttiles - 1:
            pl.when(ti < nt - 1)(lambda: wait_for(late.at[k], late_recv.at[k]))
        wait_for(halo.at[k, t], halo_recv.at[k, t])

    def update(k, t, change, scale):
        def at(f, t, c):
            if t < 0:
                return jnp.where(ti > 0, early[k, f, c], 0.0)
            if t >= ttiles:
                return jnp.where(ti < nt - 1, late[k, f, c], 0.0)
            if f < 0:
                return halo[k, t, f + REACH, c]
            if f >= ftiles:
                return halo[k, t, f - ftiles + REACH, c]
            return terms[k, at_tile(f, t), c]

        odd = lax.rem(k, 2) == 1
        for f in range(ftiles):
            i = at_tile(f, t)
            sums = [
                at(f, t, c)
                + coef[0] * (at(f - 1, t, c) + at(f + 1, t, c))
                + coef[1] * (at(f - 2, t, c) + at(f + 2, t, c))
                + coef[2] * (at(f, t - 1, c) + at(f, t + 1, c))
                for c in range(3)
            ]
            denom = sums[2] + coef[3]
            for c in range(2):
                old = gain[i, c]
                fresh = (sums[c] + prev[i, c]) / denom
                fresh = jnp.where(odd, 0.5 * (fresh + old), fresh)
                diff = fresh - old
                change = change + diff * diff
                scale = scale + fresh * fresh
                gain[i, c] = fresh
        return change, scale

    def record(k, change, scale):
        row = stats[...]
        for lane, value in ((k, change), (ITERS + k, scale)):
            total = jnp.sum(jnp.sum(value, axis=0, keepdims=True), axis=1, keepdims=True)
            row = jnp.where(lane_of == lane, total, row)
        stats[...] = row

    lane_of = lax.broadcasted_iota(jnp.int32, (1, width), 1)
    stats[...] = jnp.zeros_like(stats)
    def fetched(f, t):
        i = at_tile(f, t)
        pltpu.make_async_copy(data.at[i], data.at[i], load_sem.at[i]).wait()

    fetched(*tiles[0])

    def first_pair(p, carry):
        prepare(0, p)
        return carry

    def first_stage(n, f, t):
        total = [zero] * 3
        for p in range(blks // 2):
            total = pair_terms(f, t, p, total)
            prepare(n + 1, p)
        keep(0, f, t, total)

    lax.fori_loop(0, blks // 2, first_pair, 0)
    for copy in small:
        copy.wait()
    set_up()
    for n, (f, t) in enumerate(tiles):
        if n + 1 < len(tiles):
            fetched(*tiles[n + 1])

            first_stage(n, f, t)
        else:
            tile_terms(0, f, t)
        if n == MEET:
            pl.semaphore_wait(barrier, devices - 1)
            prior_copy.start()
        if n >= MEET:
            for f, t in tiles[(0 if n == MEET else n) : n + 1]:
                send(0, f, t)

    prior_copy.wait_recv()
    for f, t in tiles:
        i = at_tile(f, t)
        for c in range(2):
            if f == 0:
                for n in range(nb):
                    prev[i, c, n : n + 1, :] = from_prior[
                        t, c : c + 1, n * width : (n + 1) * width
                    ]
                prev[i, c] = prev[i, c] * coef[3]
            else:
                prev[i, c] = gain[at_tile(f - 1, t), c] * coef[3]

    def step(k, carry):
        change, scale = zero, zero
        for t in range(ttiles):
            arrived(k, t)
            change, scale = update(k, t, change, scale)
            for f in range(ftiles):
                tile_terms(k + 1, f, t)
                send(k + 1, f, t)
        record(k, change, scale)
        return carry

    lax.fori_loop(0, ITERS - 1, step, 0)
    change, scale = zero, zero
    for t in range(ttiles):
        arrived(ITERS - 1, t)
        change, scale = update(ITERS - 1, t, change, scale)
    record(ITERS - 1, change, scale)

    def stats_copy(step, row):
        return pltpu.make_async_remote_copy(
            src_ref=stats, dst_ref=all_stats_ref.at[row],
            send_sem=stats_send.at[0], recv_sem=stats_recv.at[0],
            device_id=peer(step), device_id_type=LOGICAL,
        )

    def send_stats(step, carry):
        stats_copy(step, me).start()
        return carry

    lax.fori_loop(1, devices, send_stats, 0, unroll=UNROLL)
    own_stats = pltpu.make_async_copy(stats, all_stats_ref.at[me], out_sem.at[1])
    own_stats.start()
    prior_copy.wait_send()
    for f, t in tiles:
        i = at_tile(f, t)
        for c in range(2):
            for n in range(nb):
                prior_ref[f, t, c : c + 1, n * width : (n + 1) * width] = gain[i, c, n : n + 1, :]
    gains_out = pltpu.make_async_copy(prior_ref, gains_ref, out_sem.at[0])
    gains_out.start()

    wait_for(halo, halo_send.at[0])
    pl.when(ti < nt - 1)(lambda: wait_for(early, early_send.at[0]))
    pl.when(ti > 0)(lambda: wait_for(late, late_send.at[0]))
    own_stats.wait()
    gains_out.wait()
    others = all_stats_ref.at[pl.ds(0, devices - 1)]
    wait_for(others, stats_send.at[0])
    wait_for(others, stats_recv.at[0])


def hand_on(gains_in, stats_in, gains_ref, changes_ref):
    gains_ref[...] = gains_in[...]
    whole = jnp.sum(stats_in[...], axis=0)
    scale = pltpu.roll(whole, whole.shape[1] - ITERS, axis=1)
    changes_ref[...] = jnp.sqrt(whole / (scale + 1e-06))[0, :ITERS]


def per_device(vis, model, block_rows, block_cols, flags, prior, couplings, damping):
    nf, nt = lax.axis_size("freq"), lax.axis_size("tm")
    ftiles, ttiles, blks = vis.shape[:3]
    width = vis.shape[-1]
    nb = prior.shape[-1] // width
    count = ftiles * ttiles
    dims = (nf, nt, ftiles, ttiles, blks, width, nb)
    vmem = pl.BlockSpec(memory_space=pltpu.VMEM)
    hbm = pl.BlockSpec(memory_space=pltpu.HBM)
    dma = pltpu.SemaphoreType.DMA
    gains, all_stats = pl.pallas_call(
        functools.partial(kernel, dims),
        name="stefcal",
        out_shape=(
            jax.ShapeDtypeStruct(prior.shape, F32),
            jax.ShapeDtypeStruct((nf * nt, 1, width), F32),
        ),
        in_specs=[hbm] * 8,
        out_specs=(hbm, hbm),
        scratch_shapes=[
            pltpu.SMEM(block_rows.shape, jnp.int32),
            pltpu.SMEM(block_rows.shape, jnp.int32),
            pltpu.SMEM(block_rows.shape, jnp.int32),
            pltpu.VMEM(prior.shape, F32),
            pltpu.VMEM(couplings.shape, F32),
            pltpu.VMEM((1, damping.shape[0]), F32),
            pltpu.VMEM((count, 2) + vis.shape[2:], BF16),
            pltpu.VMEM((count * blks, 2 * width, 2 * width), BF16),
            pltpu.VMEM((count * blks // 2, 2 * width, 2 * width), BF16),
            pltpu.VMEM((count, 2, nb, width), F32),
            pltpu.VMEM((count, 2, nb, width), F32),
            pltpu.VMEM((4, nb, width), F32),
            pltpu.VMEM(prior.shape[1:], F32),
            pltpu.VMEM((ITERS, count, 3, nb, width), F32),
            pltpu.VMEM((ITERS, ttiles, 2 * REACH, 3, nb, width), F32),
            pltpu.VMEM((ITERS, ftiles, 3, nb, width), F32),
            pltpu.VMEM((ITERS, ftiles, 3, nb, width), F32),
            pltpu.VMEM((1, width), F32),
            dma((6,)),
            dma((count,)),
            dma((2,)),
            dma((1,)),
            dma((ITERS, ttiles)),
            dma((1,)),
            dma((1,)),
            dma((ITERS,)),
            dma((ITERS,)),
            dma((1,)),
            dma((1,)),
            dma((2,)),
        ],
        compiler_params=pltpu.CompilerParams(
            collective_id=0, has_side_effects=True, vmem_limit_bytes=67043328
        ),
    )(vis, model, block_rows, block_cols, flags, prior, couplings, damping.reshape(1, -1))
    return pl.pallas_call(
        hand_on,
        name="hand_on",
        out_shape=(
            jax.ShapeDtypeStruct(prior.shape, F32),
            jax.ShapeDtypeStruct((ITERS,), F32),
        ),
        in_specs=[vmem, vmem],
        out_specs=(vmem, vmem),
    )(gains, all_stats)


def solution(mesh):
    placed = (
        P("freq", "tm", None, None, None, None),
        P("freq", "tm", None, None, None, None),
        P("freq", "tm", None),
        P("freq", "tm", None),
        P("freq", "tm", None),
        P("freq", "tm", None, None),
        P(),
        P(),
    )
    return jax.shard_map(
        per_device,
        mesh=mesh,
        in_specs=placed,
        out_specs=(P("freq", "tm", None, None), P()),
        check_vma=False,
    )
```

time: 41.2 us -> 39.7 us (0.964)
  Pallas kernels: 40.4 us -> 38.9 us
    pallas_call x1, Pallas kernels: 38.9 us -> 37.4 us  [per_device(): pl.pallas_call(functools.partial(kernel, dims), name='stefcal', out_shape...]
where the time goes in v2:
time: 39.7 us; the launch traced here: 39.5 us
  Pallas kernels  38.9 us (98%)
  between operations  0.64 us (2%)
    pallas_call x1, Pallas kernels, per_device(): pl.pallas_call(functools.partial(kernel, dims), name='stefcal', out_shape...  37.4 us
    pallas_call x1, Pallas kernels, per_device(): pl.pallas_call(hand_on, name='hand_on', out_shape=(jax.ShapeDtypeStruct(p...  1.49 us

profile of v2, /device:TPU:0, one launch (start us, length us, event | category | flops | bytes accessed | tf_op | source)
XLA Modules:
  0.0 39.5 jit_solution(961902699833467261)
XLA Ops:
  0.6 37.4 %stefcal.1 = (f32[2,2,2,2048]{3,2,1,0:T(2,128)}, f32[32,1,128]{2,1,0:T(1,128)}) custom-call(bf16[2,2,16,2,128,128]{5,4,3,2,1,0:T(8,128)(2,1)} %vis_ref.1, bf16[2,2,16,2,128,128]{5,4,3,2,1,0:T(8,128)(2,1)} %model_ref.1, s32[2,2,16]{2,1,0:T(2,128)} %rows_in.1, s32[2,2,16]{2,1,0:T(2,128)} %cols_in.1, s32[2,2,16]{2,1,0:T(2,128)} %flags_in.1, ...), custom_call_target="tpu_custom_call" | custom-call | tf_op jit(solution)/shard_map/stefcal/pallas_call | solution.py:369
  38.0 1.5 %hand_on.1 = (f32[2,2,2,2048]{3,2,1,0:T(2,128)}, f32[4]{0:T(128)}) custom-call(f32[2,2,2,2048]{3,2,1,0:T(2,128)} %get-tuple-element.4.gains_in, f32[32,1,128]{2,1,0:T(1,128)} %get-tuple-element.5.stats_in), custom_call_target="tpu_custom_call" | custom-call | tf_op jit(solution)/shard_map/hand_on/pallas_call | solution.py:414

commit v3 on v2

--- a/solution.py
+++ b/solution.py
@@ -9,8 +9,11 @@
 
 ITERS = 4
 REACH = 2
-MEET = 0
+EARLY = 2
 UNROLL = 8
+CHUNK = 16
+VPU_PART = (0, 16)
+PARTS = 4
 MESH = pl.DeviceIdType.MESH
 LOGICAL = pl.DeviceIdType.LOGICAL
 F32 = jnp.float32
@@ -27,16 +30,18 @@
     vis_ref, model_ref, rows_in, cols_in, flags_in, prior_in, coup_in, damp_in,
     gains_ref, all_stats_ref,
     rows_ref, cols_ref, flags_ref, prior_ref, coup_ref, damp_ref,
-    data, wa, wb, gain, prev, coef, from_prior, terms, halo, early, late,
+    data, wa, wb, cv, gain, prev, coef, from_prior, terms, halo, early, late,
     stats,
     small_sem, load_sem, prior_sem, halo_send, halo_recv,
     early_send, late_send, early_recv, late_recv, stats_send, stats_recv, out_sem,
 ):
-    nf, nt, ftiles, ttiles, blks, width, nb = dims
+    nf, nt, ftiles, ttiles, blks, width, nb, on_mxu = dims
+    on_vpu = blks - on_mxu
     fi = lax.axis_index("freq")
     ti = lax.axis_index("tm")
     above, below = lax.rem(fi + 1, nf), lax.rem(fi + nf - 1, nf)
-    tiles = [(f, t) for t in range(ttiles) for f in range(ftiles)]
+    order = range(ftiles - 1, -1, -1)
+    tiles = [(f, t) for t in range(ttiles) for f in order]
 
     def at_tile(f, t):
         return t * ftiles + f
@@ -47,15 +52,22 @@
     def peer(step):
         return lax.rem(me + step, devices)
 
-    def loads(f, t):
-        i = at_tile(f, t)
-        return (
-            pltpu.make_async_copy(vis_ref.at[f, t], data.at[i, 0], load_sem.at[i]),
-            pltpu.make_async_copy(model_ref.at[f, t], data.at[i, 1], load_sem.at[i]),
-        )
-
-    for copy in loads(*tiles[0]):
-        copy.start()
+    def load(f, t, part):
+        i, size = at_tile(f, t), blks // PARTS
+        some = pl.ds(part * size, size)
+        for n, ref in enumerate((vis_ref, model_ref)):
+            pltpu.make_async_copy(
+                ref.at[f, t, some], data.at[i, n, some], load_sem.at[i, part]
+            ).start()
+
+    def loaded(f, t, part):
+        i, size = at_tile(f, t), blks // PARTS
+        some = pl.ds(part * size, size)
+        wait_for(data.at[i, :, some], load_sem.at[i, part])
+
+    def wait_for(ref, sem):
+        pltpu.make_async_copy(ref, ref, sem).wait()
+
     small = [
         pltpu.make_async_copy(src, dst, small_sem.at[n])
         for n, (src, dst) in enumerate((
@@ -65,9 +77,9 @@
     ]
     for copy in small:
         copy.start()
-    for f, t in tiles[1:]:
-        for copy in loads(f, t):
-            copy.start()
+    for f, t in tiles[:2]:
+        for part in range(PARTS):
+            load(f, t, part)
 
     barrier = pltpu.get_barrier_semaphore()
 
@@ -97,14 +109,14 @@
     def up_copy(k, f, t):
         return pltpu.make_async_remote_copy(
             src_ref=terms.at[k, at_tile(f, t)], dst_ref=halo.at[k, t, f - (ftiles - REACH)],
-            send_sem=halo_send.at[0], recv_sem=halo_recv.at[k, t],
+            send_sem=halo_send.at[0], recv_sem=halo_recv.at[k, t, int(f == ftiles - REACH)],
             device_id={"freq": above}, device_id_type=MESH,
         )
 
     def down_copy(k, f, t):
         return pltpu.make_async_remote_copy(
             src_ref=terms.at[k, at_tile(f, t)], dst_ref=halo.at[k, t, REACH + f],
-            send_sem=halo_send.at[0], recv_sem=halo_recv.at[k, t],
+            send_sem=halo_send.at[0], recv_sem=halo_recv.at[k, t, 0],
             device_id={"freq": below}, device_id_type=MESH,
         )
 
@@ -122,39 +134,62 @@
             device_id={"tm": lax.rem(ti + nt - 1, nt)}, device_id_type=MESH,
         )
 
-    def wait_for(ref, sem):
-        pltpu.make_async_copy(ref, ref, sem).wait()
-
-    def prepare(i, p):
+    def prepare(i, b, slot, side):
+        for r in range(0, width, CHUNK):
+            at = pl.ds(r, CHUNK)
+            v_re = data[i, 0, b, 0, at].astype(F32)
+            v_im = data[i, 0, b, 1, at].astype(F32)
+            m_re = data[i, 1, b, 0, at].astype(F32)
+            m_im = data[i, 1, b, 1, at].astype(F32)
+            re = v_re * m_re + v_im * m_im
+            im = v_re * m_im - v_im * m_re
+            sq = m_re * m_re + m_im * m_im
+            if side is None:
+                for c, value in enumerate((re, im, sq)):
+                    cv[i, slot, c, at] = value
+                continue
+            lower = pl.ds(width + r, CHUNK)
+            wa[i, 2 * slot + side, 0, at], wb[i, slot, side, at] = split(re)
+            wa[i, 2 * slot + side, 0, lower], wb[i, slot, side, lower] = split(im)
+            wa[i, 2 * slot + side, 1, at], wa[i, 2 * slot + side, 1, lower] = split(sq)
+
+    def prepare_pair(i, p):
         for side in range(2):
-            b = 2 * p + side
-            lo = side * width
-            v_re = data[i, 0, b, 0].astype(F32)
-            v_im = data[i, 0, b, 1].astype(F32)
-            m_re = data[i, 1, b, 0].astype(F32)
-            m_im = data[i, 1, b, 1].astype(F32)
-            re_hi, re_lo = split(v_re * m_re + v_im * m_im)
-            im_hi, im_lo = split(v_re * m_im - v_im * m_re)
-            sq_hi, sq_lo = split(m_re * m_re + m_im * m_im)
-            wa[i * blks + b, 0:width, 0:width] = re_hi
-            wa[i * blks + b, width:, 0:width] = im_hi
-            wa[i * blks + b, 0:width, width:] = sq_hi
-            wa[i * blks + b, width:, width:] = sq_lo
-            wb[i * (blks // 2) + p, 0:width, lo : lo + width] = re_lo
-            wb[i * (blks // 2) + p, width:, lo : lo + width] = im_lo
+            prepare(i, 2 * p + side, p, side)
+
+    def prepare_tile(i, part):
+        def pair(p, carry):
+            prepare_pair(i, p)
+            return carry
+
+        size = blks // 2 // PARTS
+        lax.fori_loop(part * size, part * size + size, pair, 0)
 
     row_of = lax.broadcasted_iota(jnp.int32, (8, width), 0)
     block_of = lax.broadcasted_iota(jnp.int32, (nb, width), 0)
     zero = jnp.zeros((nb, width), F32)
 
+    def column(f, t, b):
+        return jnp.where(flags_ref[f, t, b] != 0, cols_ref[f, t, b], -1)
+
+    def gains_of(f, t, b):
+        row, i = rows_ref[f, t, b], at_tile(f, t)
+        return gain[i, 0, pl.ds(row, 1), :], gain[i, 1, pl.ds(row, 1), :]
+
+    def add(total, col, parts):
+        hit = block_of == col
+        return [
+            acc + jnp.where(hit, jnp.broadcast_to(one, (nb, width)), 0.0)
+            for acc, one in zip(total, parts)
+        ]
+
     def pair_terms(f, t, p, total):
         i = at_tile(f, t)
         highs, outs, cols = [], [], []
-        for b in (2 * p, 2 * p + 1):
-            row = rows_ref[f, t, b]
-            cols.append(jnp.where(flags_ref[f, t, b] != 0, cols_ref[f, t, b], -1))
-            re = jnp.broadcast_to(gain[i, 0, pl.ds(row, 1), :], (8, width))
-            im = jnp.broadcast_to(gain[i, 1, pl.ds(row, 1), :], (8, width))
+        for side in range(2):
+            b = 2 * p + side
+            cols.append(column(f, t, b))
+            re, im = (jnp.broadcast_to(x, (8, width)) for x in gains_of(f, t, b))
             sq = re * re + im * im
             left = jnp.where(row_of == 0, re, jnp.where(row_of == 1, im, sq))
             right = jnp.where(row_of == 0, -im, jnp.where(row_of == 1, re, sq))
@@ -162,24 +197,43 @@
             lhs_hi = lhs.astype(BF16).astype(F32)
             highs.append(lhs_hi)
             lhs = jnp.concatenate([lhs_hi, lhs - lhs_hi], axis=0).astype(BF16)
-            out = jnp.dot(lhs, wa[i * blks + b], preferred_element_type=F32)
+            rhs = jnp.concatenate([wa[i, b, 0], wa[i, b, 1]], axis=1)
+            out = jnp.dot(lhs, rhs, preferred_element_type=F32)
             outs.append(out[0:8] + out[8:16])
         low_out = jnp.dot(
             jnp.concatenate(highs, axis=0).astype(BF16),
-            wb[i * (blks // 2) + p],
+            jnp.concatenate([wb[i, p, 0], wb[i, p, 1]], axis=1),
             preferred_element_type=F32,
         )
         low_outs = (low_out[0:8, 0:width], low_out[8:16, width:])
         for out, low_out, col in zip(outs, low_outs, cols):
             num = out[:, 0:width] + low_out
-            den = out[:, width:]
-            hit = block_of == col
-            parts = (num[0:1], num[1:2], den[2:3])
-            total = [
-                acc + jnp.where(hit, jnp.broadcast_to(one, (nb, width)), 0.0)
-                for acc, one in zip(total, parts)
-            ]
+            total = add(total, col, (num[0:1], num[1:2], out[2:3, width:]))
         return total
+
+    def spread(f, t):
+        rows = [gains_of(f, t, on_mxu + v) for v in range(on_vpu)]
+        pad = [jnp.zeros((-on_vpu % 8, width), F32)] if on_vpu % 8 else []
+        re, im = (jnp.concatenate([x[c] for x in rows] + pad, axis=0) for c in range(2))
+        return jnp.concatenate([re, im, re * re + im * im], axis=0).T, re.shape[0]
+
+    def plain_terms(f, t, v, turned, total):
+        across, apart = turned
+        i = at_tile(f, t)
+        sums = [jnp.zeros((8, width), F32)] * 3
+        for r in range(0, width, 8):
+            g_re, g_im, g_sq = (
+                jnp.broadcast_to(
+                    across[r : r + 8, c * apart + v : c * apart + v + 1], (8, width)
+                )
+                for c in range(3)
+            )
+            re, im, sq = (cv[i, v, c, r : r + 8] for c in range(3))
+            sums[0] = sums[0] + (re * g_re - im * g_im)
+            sums[1] = sums[1] + (im * g_re + re * g_im)
+            sums[2] = sums[2] + sq * g_sq
+        parts = [jnp.sum(x, axis=0, keepdims=True) for x in sums]
+        return add(total, column(f, t, on_mxu + v), parts)
 
     def keep(k, f, t, total):
         for c in range(3):
@@ -187,28 +241,52 @@
 
     def tile_terms(k, f, t):
         total = [zero] * 3
-        for p in range(blks // 2):
-            total = pair_terms(f, t, p, total)
+        turned = spread(f, t) if on_vpu else None
+        for n in range(max(on_mxu // 2, on_vpu)):
+            if n < on_mxu // 2:
+                total = pair_terms(f, t, n, total)
+            if n < on_vpu:
+                total = plain_terms(f, t, n, turned, total)
         keep(k, f, t, total)
+
+    def first_stage(n, f, t):
+        for part in range(PARTS):
+            prepare_tile(at_tile(*tiles[n + 1]), part)
+        tile_terms(0, f, t)
+
+    outer = lax.rem(fi, 2) == 1
+
+    def send_up(k, f, t):
+        if f >= ftiles - REACH:
+            up_copy(k, f, t).start()
+
+    def send_down(k, f, t):
+        if f < REACH:
+            down_copy(k, f, t).start()
 
     def send(k, f, t):
         if t == ttiles - 1:
             pl.when(ti < nt - 1)(later_copy(k, f).start)
         if t == 0:
             pl.when(ti > 0)(earlier_copy(k, f).start)
-        if f >= ftiles - REACH:
-            up_copy(k, f, t).start()
-        if f < REACH:
-            down_copy(k, f, t).start()
-
-    def arrived(k, t):
-        if t == 0:
-            pl.when(ti > 0)(lambda: wait_for(early.at[k], early_recv.at[k]))
-        if t == ttiles - 1:
-            pl.when(ti < nt - 1)(lambda: wait_for(late.at[k], late_recv.at[k]))
-        wait_for(halo.at[k, t], halo_recv.at[k, t])
-
-    def update(k, t, change, scale):
+        pl.when(outer)(lambda: send_up(k, f, t))
+        pl.when(jnp.logical_not(outer))(lambda: send_down(k, f, t))
+
+    def send_rest(k, f, t):
+        pl.when(outer)(lambda: send_down(k, f, t))
+        pl.when(jnp.logical_not(outer))(lambda: send_up(k, f, t))
+
+    def arrived(k, f, t):
+        if f == ftiles - 1:
+            if t == 0:
+                pl.when(ti > 0)(lambda: wait_for(early.at[k], early_recv.at[k]))
+            if t == ttiles - 1:
+                pl.when(ti < nt - 1)(lambda: wait_for(late.at[k], late_recv.at[k]))
+            wait_for(halo.at[k, t, pl.ds(1, 2 * REACH - 1)], halo_recv.at[k, t, 0])
+        if f == 0:
+            wait_for(halo.at[k, t, 0], halo_recv.at[k, t, 1])
+
+    def update(k, f, t, change, scale):
         def at(f, t, c):
             if t < 0:
                 return jnp.where(ti > 0, early[k, f, c], 0.0)
@@ -221,24 +299,23 @@
             return terms[k, at_tile(f, t), c]
 
         odd = lax.rem(k, 2) == 1
-        for f in range(ftiles):
-            i = at_tile(f, t)
-            sums = [
-                at(f, t, c)
-                + coef[0] * (at(f - 1, t, c) + at(f + 1, t, c))
-                + coef[1] * (at(f - 2, t, c) + at(f + 2, t, c))
-                + coef[2] * (at(f, t - 1, c) + at(f, t + 1, c))
-                for c in range(3)
-            ]
-            denom = sums[2] + coef[3]
-            for c in range(2):
-                old = gain[i, c]
-                fresh = (sums[c] + prev[i, c]) / denom
-                fresh = jnp.where(odd, 0.5 * (fresh + old), fresh)
-                diff = fresh - old
-                change = change + diff * diff
-                scale = scale + fresh * fresh
-                gain[i, c] = fresh
+        i = at_tile(f, t)
+        sums = [
+            at(f, t, c)
+            + coef[0] * (at(f - 1, t, c) + at(f + 1, t, c))
+            + coef[1] * (at(f - 2, t, c) + at(f + 2, t, c))
+            + coef[2] * (at(f, t - 1, c) + at(f, t + 1, c))
+            for c in range(3)
+        ]
+        denom = sums[2] + coef[3]
+        for c in range(2):
+            old = gain[i, c]
+            fresh = (sums[c] + prev[i, c]) / denom
+            fresh = jnp.where(odd, 0.5 * (fresh + old), fresh)
+            diff = fresh - old
+            change = change + diff * diff
+            scale = scale + fresh * fresh
+            gain[i, c] = fresh
         return change, scale
 
     def record(k, change, scale):
@@ -250,70 +327,86 @@
 
     lane_of = lax.broadcasted_iota(jnp.int32, (1, width), 1)
     stats[...] = jnp.zeros_like(stats)
-    def fetched(f, t):
-        i = at_tile(f, t)
-        pltpu.make_async_copy(data.at[i], data.at[i], load_sem.at[i]).wait()
-
-    fetched(*tiles[0])
-
-    def first_pair(p, carry):
-        prepare(0, p)
-        return carry
-
-    def first_stage(n, f, t):
-        total = [zero] * 3
-        for p in range(blks // 2):
-            total = pair_terms(f, t, p, total)
-            prepare(n + 1, p)
-        keep(0, f, t, total)
-
-    lax.fori_loop(0, blks // 2, first_pair, 0)
+    for part in range(PARTS):
+        loaded(*tiles[0], part)
+        if len(tiles) > 2:
+            load(*tiles[2], part)
+        prepare_tile(at_tile(*tiles[0]), part)
     for copy in small:
         copy.wait()
     set_up()
+    last = len(tiles) - 1
+    ahead = me < EARLY
+
+    def meet(n, ready):
+        def go():
+            pl.semaphore_wait(barrier, devices - 1)
+
+        def pass_on(some):
+            for f, t in some:
+                send(0, f, t)
+                send_rest(0, f, t)
+
+        @pl.when(jnp.logical_not(ahead))
+        def _():
+            if n == 0:
+                go()
+            pass_on(ready)
+            if n == 0:
+                prior_copy.start()
+
+        if n == last:
+            @pl.when(ahead)
+            def _():
+                go()
+                pass_on(tiles)
+                prior_copy.start()
+
     for n, (f, t) in enumerate(tiles):
         if n + 1 < len(tiles):
-            fetched(*tiles[n + 1])
-
+            for part in range(PARTS):
+                loaded(*tiles[n + 1], part)
+                if n + 3 < len(tiles):
+                    load(*tiles[n + 3], part)
             first_stage(n, f, t)
         else:
             tile_terms(0, f, t)
-        if n == MEET:
-            pl.semaphore_wait(barrier, devices - 1)
-            prior_copy.start()
-        if n >= MEET:
-            for f, t in tiles[(0 if n == MEET else n) : n + 1]:
-                send(0, f, t)
-
-    prior_copy.wait_recv()
+        meet(n, [(f, t)])
+
     for f, t in tiles:
-        i = at_tile(f, t)
-        for c in range(2):
-            if f == 0:
+        if f > 0:
+            for c in range(2):
+                prev[at_tile(f, t), c] = gain[at_tile(f - 1, t), c] * coef[3]
+
+    def take_prior():
+        prior_copy.wait_recv()
+        for t in range(ttiles):
+            i = at_tile(0, t)
+            for c in range(2):
                 for n in range(nb):
                     prev[i, c, n : n + 1, :] = from_prior[
                         t, c : c + 1, n * width : (n + 1) * width
                     ]
                 prev[i, c] = prev[i, c] * coef[3]
-            else:
-                prev[i, c] = gain[at_tile(f - 1, t), c] * coef[3]
 
     def step(k, carry):
         change, scale = zero, zero
-        for t in range(ttiles):
-            arrived(k, t)
-            change, scale = update(k, t, change, scale)
-            for f in range(ftiles):
-                tile_terms(k + 1, f, t)
-                send(k + 1, f, t)
+        for f, t in tiles:
+            arrived(k, f, t)
+            if f == 0 and t == 0:
+                pl.when(k == 0)(take_prior)
+            change, scale = update(k, f, t, change, scale)
+            tile_terms(k + 1, f, t)
+            send(k + 1, f, t)
+            send_rest(k + 1, f, t)
         record(k, change, scale)
         return carry
 
     lax.fori_loop(0, ITERS - 1, step, 0)
     change, scale = zero, zero
-    for t in range(ttiles):
-        arrived(ITERS - 1, t)
-        change, scale = update(ITERS - 1, t, change, scale)
+    for f, t in tiles:
+        arrived(ITERS - 1, f, t)
+        change, scale = update(ITERS - 1, f, t, change, scale)
     record(ITERS - 1, change, scale)
 
     def stats_copy(step, row):
@@ -362,7 +455,10 @@
     width = vis.shape[-1]
     nb = prior.shape[-1] // width
     count = ftiles * ttiles
-    dims = (nf, nt, ftiles, ttiles, blks, width, nb)
+    on_vpu = VPU_PART[0] * blks // VPU_PART[1]
+    on_mxu = blks - on_vpu
+    assert on_mxu % 2 == 0
+    dims = (nf, nt, ftiles, ttiles, blks, width, nb, on_mxu)
     vmem = pl.BlockSpec(memory_space=pltpu.VMEM)
     hbm = pl.BlockSpec(memory_space=pltpu.HBM)
     dma = pltpu.SemaphoreType.DMA
@@ -383,8 +479,9 @@
             pltpu.VMEM(couplings.shape, F32),
             pltpu.VMEM((1, damping.shape[0]), F32),
             pltpu.VMEM((count, 2) + vis.shape[2:], BF16),
-            pltpu.VMEM((count * blks, 2 * width, 2 * width), BF16),
-            pltpu.VMEM((count * blks // 2, 2 * width, 2 * width), BF16),
+            pltpu.VMEM((count, on_mxu, 2, 2 * width, width), BF16),
+            pltpu.VMEM((count, on_mxu // 2, 2, 2 * width, width), BF16),
+            pltpu.VMEM((count, max(on_vpu, 1), 3, width, width), F32),
             pltpu.VMEM((count, 2, nb, width), F32),
             pltpu.VMEM((count, 2, nb, width), F32),
             pltpu.VMEM((4, nb, width), F32),
@@ -395,10 +492,10 @@
             pltpu.VMEM((ITERS, ftiles, 3, nb, width), F32),
             pltpu.VMEM((1, width), F32),
             dma((6,)),
-            dma((count,)),
+            dma((count, PARTS)),
             dma((2,)),
             dma((1,)),
-            dma((ITERS, ttiles)),
+            dma((ITERS, ttiles, 2)),
             dma((1,)),
             dma((1,)),
             dma((ITERS,)),

time: 39.7 us -> 37.3 us (0.940)
  Pallas kernels: 38.9 us -> 36.5 us
    pallas_call x1, Pallas kernels: 37.4 us -> 35 us  [per_device(): pl.pallas_call(functools.partial(kernel, dims), name='stefcal', out_shape...]
where the time goes in v3:
time: 37.3 us; the launch traced here: 37.2 us
  Pallas kernels  36.5 us (98%)
  between operations  0.64 us (2%)
    pallas_call x1, Pallas kernels, per_device(): pl.pallas_call(functools.partial(kernel, dims), name='stefcal', out_shape...  35 us
    pallas_call x1, Pallas kernels, per_device(): pl.pallas_call(hand_on, name='hand_on', out_shape=(jax.ShapeDtypeStruct(p...  1.49 us

profile of v3, /device:TPU:0, one launch (start us, length us, event | category | flops | bytes accessed | tf_op | source)
XLA Modules:
  0.0 37.2 jit_solution(11214460751383964456)
XLA Ops:
  0.6 35.0 %stefcal.1 = (f32[2,2,2,2048]{3,2,1,0:T(2,128)}, f32[32,1,128]{2,1,0:T(1,128)}) custom-call(bf16[2,2,16,2,128,128]{5,4,3,2,1,0:T(8,128)(2,1)} %vis_ref.1, bf16[2,2,16,2,128,128]{5,4,3,2,1,0:T(8,128)(2,1)} %model_ref.1, s32[2,2,16]{2,1,0:T(2,128)} %rows_in.1, s32[2,2,16]{2,1,0:T(2,128)} %cols_in.1, s32[2,2,16]{2,1,0:T(2,128)} %flags_in.1, ...), custom_call_target="tpu_custom_call" | custom-call | tf_op jit(solution)/shard_map/stefcal/pallas_call | solution.py:465
  35.7 1.5 %hand_on.1 = (f32[2,2,2,2048]{3,2,1,0:T(2,128)}, f32[4]{0:T(128)}) custom-call(f32[2,2,2,2048]{3,2,1,0:T(2,128)} %get-tuple-element.4.gains_in, f32[32,1,128]{2,1,0:T(1,128)} %get-tuple-element.5.stats_in), custom_call_target="tpu_custom_call" | custom-call | tf_op jit(solution)/shard_map/hand_on/pallas_call | solution.py:511

commit v4 on v3

--- a/solution.py
+++ b/solution.py
@@ -12,7 +12,6 @@
 EARLY = 2
 UNROLL = 8
 CHUNK = 16
-VPU_PART = (0, 16)
 PARTS = 4
 MESH = pl.DeviceIdType.MESH
 LOGICAL = pl.DeviceIdType.LOGICAL
@@ -30,13 +29,12 @@
     vis_ref, model_ref, rows_in, cols_in, flags_in, prior_in, coup_in, damp_in,
     gains_ref, all_stats_ref,
     rows_ref, cols_ref, flags_ref, prior_ref, coup_ref, damp_ref,
-    data, wa, wb, cv, gain, prev, coef, from_prior, terms, halo, early, late,
+    data, wa, wb, gain, prev, coef, from_prior, terms, halo, early, late,
     stats,
     small_sem, load_sem, prior_sem, halo_send, halo_recv,
     early_send, late_send, early_recv, late_recv, stats_send, stats_recv, out_sem,
 ):
-    nf, nt, ftiles, ttiles, blks, width, nb, on_mxu = dims
-    on_vpu = blks - on_mxu
+    nf, nt, ftiles, ttiles, blks, width, nb = dims
     fi = lax.axis_index("freq")
     ti = lax.axis_index("tm")
     above, below = lax.rem(fi + 1, nf), lax.rem(fi + nf - 1, nf)
@@ -144,10 +142,6 @@
             re = v_re * m_re + v_im * m_im
             im = v_re * m_im - v_im * m_re
             sq = m_re * m_re + m_im * m_im
-            if side is None:
-                for c, value in enumerate((re, im, sq)):
-                    cv[i, slot, c, at] = value
-                continue
             lower = pl.ds(width + r, CHUNK)
             wa[i, 2 * slot + side, 0, at], wb[i, slot, side, at] = split(re)
             wa[i, 2 * slot + side, 0, lower], wb[i, slot, side, lower] = split(im)
@@ -211,48 +205,15 @@
             total = add(total, col, (num[0:1], num[1:2], out[2:3, width:]))
         return total
 
-    def spread(f, t):
-        rows = [gains_of(f, t, on_mxu + v) for v in range(on_vpu)]
-        pad = [jnp.zeros((-on_vpu % 8, width), F32)] if on_vpu % 8 else []
-        re, im = (jnp.concatenate([x[c] for x in rows] + pad, axis=0) for c in range(2))
-        return jnp.concatenate([re, im, re * re + im * im], axis=0).T, re.shape[0]
-
-    def plain_terms(f, t, v, turned, total):
-        across, apart = turned
-        i = at_tile(f, t)
-        sums = [jnp.zeros((8, width), F32)] * 3
-        for r in range(0, width, 8):
-            g_re, g_im, g_sq = (
-                jnp.broadcast_to(
-                    across[r : r + 8, c * apart + v : c * apart + v + 1], (8, width)
-                )
-                for c in range(3)
-            )
-            re, im, sq = (cv[i, v, c, r : r + 8] for c in range(3))
-            sums[0] = sums[0] + (re * g_re - im * g_im)
-            sums[1] = sums[1] + (im * g_re + re * g_im)
-            sums[2] = sums[2] + sq * g_sq
-        parts = [jnp.sum(x, axis=0, keepdims=True) for x in sums]
-        return add(total, column(f, t, on_mxu + v), parts)
-
     def keep(k, f, t, total):
         for c in range(3):
             terms[k, at_tile(f, t), c] = total[c]
 
     def tile_terms(k, f, t):
         total = [zero] * 3
-        turned = spread(f, t) if on_vpu else None
-        for n in range(max(on_mxu // 2, on_vpu)):
-            if n < on_mxu // 2:
-                total = pair_terms(f, t, n, total)
-            if n < on_vpu:
-                total = plain_terms(f, t, n, turned, total)
+        for p in range(blks // 2):
+            total = pair_terms(f, t, p, total)
         keep(k, f, t, total)
-
-    def first_stage(n, f, t):
-        for part in range(PARTS):
-            prepare_tile(at_tile(*tiles[n + 1]), part)
-        tile_terms(0, f, t)
 
     outer = lax.rem(fi, 2) == 1
 
@@ -363,14 +324,13 @@
                 prior_copy.start()
 
     for n, (f, t) in enumerate(tiles):
-        if n + 1 < len(tiles):
+        if n > 0:
             for part in range(PARTS):
-                loaded(*tiles[n + 1], part)
-                if n + 3 < len(tiles):
-                    load(*tiles[n + 3], part)
-            first_stage(n, f, t)
-        else:
-            tile_terms(0, f, t)
+                loaded(f, t, part)
+                if n + 2 < len(tiles):
+                    load(*tiles[n + 2], part)
+                prepare_tile(at_tile(f, t), part)
+        tile_terms(0, f, t)
         meet(n, [(f, t)])
 
     for f, t in tiles:
@@ -455,10 +415,7 @@
     width = vis.shape[-1]
     nb = prior.shape[-1] // width
     count = ftiles * ttiles
-    on_vpu = VPU_PART[0] * blks // VPU_PART[1]
-    on_mxu = blks - on_vpu
-    assert on_mxu % 2 == 0
-    dims = (nf, nt, ftiles, ttiles, blks, width, nb, on_mxu)
+    dims = (nf, nt, ftiles, ttiles, blks, width, nb)
     vmem = pl.BlockSpec(memory_space=pltpu.VMEM)
     hbm = pl.BlockSpec(memory_space=pltpu.HBM)
     dma = pltpu.SemaphoreType.DMA
@@ -479,9 +436,8 @@
             pltpu.VMEM(couplings.shape, F32),
             pltpu.VMEM((1, damping.shape[0]), F32),
             pltpu.VMEM((count, 2) + vis.shape[2:], BF16),
-            pltpu.VMEM((count, on_mxu, 2, 2 * width, width), BF16),
-            pltpu.VMEM((count, on_mxu // 2, 2, 2 * width, width), BF16),
-            pltpu.VMEM((count, max(on_vpu, 1), 3, width, width), F32),
+            pltpu.VMEM((count, blks, 2, 2 * width, width), BF16),
+            pltpu.VMEM((count, blks // 2, 2, 2 * width, width), BF16),
             pltpu.VMEM((count, 2, nb, width), F32),
             pltpu.VMEM((count, 2, nb, width), F32),
             pltpu.VMEM((4, nb, width), F32),

time: 37.3 us -> 37.1 us (level)
  no operation moved by 1% of the time
where the time goes in v4:
time: 37.1 us; the launch traced here: 36.9 us
  Pallas kernels  36.3 us (98%)
  between operations  0.64 us (2%)
    pallas_call x1, Pallas kernels, per_device(): pl.pallas_call(functools.partial(kernel, dims), name='stefcal', out_shape...  34.8 us
    pallas_call x1, Pallas kernels, per_device(): pl.pallas_call(hand_on, name='hand_on', out_shape=(jax.ShapeDtypeStruct(p...  1.49 us

profile of v4, /device:TPU:0, one launch (start us, length us, event | category | flops | bytes accessed | tf_op | source)
XLA Modules:
  0.0 36.9 jit_solution(3092037891384426690)
XLA Ops:
  0.6 34.8 %stefcal.1 = (f32[2,2,2,2048]{3,2,1,0:T(2,128)}, f32[32,1,128]{2,1,0:T(1,128)}) custom-call(bf16[2,2,16,2,128,128]{5,4,3,2,1,0:T(8,128)(2,1)} %vis_ref.1, bf16[2,2,16,2,128,128]{5,4,3,2,1,0:T(8,128)(2,1)} %model_ref.1, s32[2,2,16]{2,1,0:T(2,128)} %rows_in.1, s32[2,2,16]{2,1,0:T(2,128)} %cols_in.1, s32[2,2,16]{2,1,0:T(2,128)} %flags_in.1, ...), custom_call_target="tpu_custom_call" | custom-call | tf_op jit(solution)/shard_map/stefcal/pallas_call | solution.py:422
  35.4 1.5 %hand_on.1 = (f32[2,2,2,2048]{3,2,1,0:T(2,128)}, f32[4]{0:T(128)}) custom-call(f32[2,2,2,2048]{3,2,1,0:T(2,128)} %get-tuple-element.4.gains_in, f32[32,1,128]{2,1,0:T(1,128)} %get-tuple-element.5.stats_in), custom_call_target="tpu_custom_call" | custom-call | tf_op jit(solution)/shard_map/hand_on/pallas_call | solution.py:467

commit v5 on v4

--- a/solution.py
+++ b/solution.py
@@ -10,7 +10,7 @@
 ITERS = 4
 REACH = 2
 EARLY = 2
-UNROLL = 8
+UNROLL = 31
 CHUNK = 16
 PARTS = 4
 MESH = pl.DeviceIdType.MESH
@@ -50,18 +50,21 @@
     def peer(step):
         return lax.rem(me + step, devices)
 
+    def parts(f, t):
+        return PARTS if (f, t) == tiles[0] else 1
+
     def load(f, t, part):
-        i, size = at_tile(f, t), blks // PARTS
+        i, size = at_tile(f, t), blks // parts(f, t)
         some = pl.ds(part * size, size)
         for n, ref in enumerate((vis_ref, model_ref)):
             pltpu.make_async_copy(
-                ref.at[f, t, some], data.at[i, n, some], load_sem.at[i, part]
+                ref.at[f, t, some], data.at[i, n, some], load_sem.at[part if (f, t) == tiles[0] else PARTS + i]
             ).start()
 
     def loaded(f, t, part):
-        i, size = at_tile(f, t), blks // PARTS
+        i, size = at_tile(f, t), blks // parts(f, t)
         some = pl.ds(part * size, size)
-        wait_for(data.at[i, :, some], load_sem.at[i, part])
+        wait_for(data.at[i, :, some], load_sem.at[part if (f, t) == tiles[0] else PARTS + i])
 
     def wait_for(ref, sem):
         pltpu.make_async_copy(ref, ref, sem).wait()
@@ -76,7 +79,7 @@
     for copy in small:
         copy.start()
     for f, t in tiles[:2]:
-        for part in range(PARTS):
+        for part in range(parts(f, t)):
             load(f, t, part)
 
     barrier = pltpu.get_barrier_semaphore()
@@ -151,12 +154,12 @@
         for side in range(2):
             prepare(i, 2 * p + side, p, side)
 
-    def prepare_tile(i, part):
+    def prepare_tile(i, part, count):
         def pair(p, carry):
             prepare_pair(i, p)
             return carry
 
-        size = blks // 2 // PARTS
+        size = blks // 2 // count
         lax.fori_loop(part * size, part * size + size, pair, 0)
 
     row_of = lax.broadcasted_iota(jnp.int32, (8, width), 0)
@@ -290,9 +293,9 @@
     stats[...] = jnp.zeros_like(stats)
     for part in range(PARTS):
         loaded(*tiles[0], part)
-        if len(tiles) > 2:
-            load(*tiles[2], part)
-        prepare_tile(at_tile(*tiles[0]), part)
+        if part == 0 and len(tiles) > 2:
+            load(*tiles[2], 0)
+        prepare_tile(at_tile(*tiles[0]), part, PARTS)
     for copy in small:
         copy.wait()
     set_up()
@@ -325,11 +328,10 @@
 
     for n, (f, t) in enumerate(tiles):
         if n > 0:
-            for part in range(PARTS):
-                loaded(f, t, part)
-                if n + 2 < len(tiles):
-                    load(*tiles[n + 2], part)
-                prepare_tile(at_tile(f, t), part)
+            loaded(f, t, 0)
+            if n + 2 < len(tiles):
+                load(*tiles[n + 2], 0)
+            prepare_tile(at_tile(f, t), 0, 1)
         tile_terms(0, f, t)
         meet(n, [(f, t)])
 
@@ -448,7 +450,7 @@
             pltpu.VMEM((ITERS, ftiles, 3, nb, width), F32),
             pltpu.VMEM((1, width), F32),
             dma((6,)),
-            dma((count, PARTS)),
+            dma((PARTS + count,)),
             dma((2,)),
             dma((1,)),
             dma((ITERS, ttiles, 2)),

time: 37.1 us -> 37 us (level)
  no operation moved by 1% of the time
where the time goes in v5:
time: 37 us; the launch traced here: 36.8 us
  Pallas kernels  36.2 us (98%)
  between operations  0.64 us (2%)
    pallas_call x1, Pallas kernels, per_device(): pl.pallas_call(functools.partial(kernel, dims), name='stefcal', out_shape...  34.7 us
    pallas_call x1, Pallas kernels, per_device(): pl.pallas_call(hand_on, name='hand_on', out_shape=(jax.ShapeDtypeStruct(p...  1.49 us

profile of v5, /device:TPU:0, one launch (start us, length us, event | category | flops | bytes accessed | tf_op | source)
XLA Modules:
  0.0 36.8 jit_solution(14335541173962140683)
XLA Ops:
  0.6 34.7 %stefcal.1 = (f32[2,2,2,2048]{3,2,1,0:T(2,128)}, f32[32,1,128]{2,1,0:T(1,128)}) custom-call(bf16[2,2,16,2,128,128]{5,4,3,2,1,0:T(8,128)(2,1)} %vis_ref.1, bf16[2,2,16,2,128,128]{5,4,3,2,1,0:T(8,128)(2,1)} %model_ref.1, s32[2,2,16]{2,1,0:T(2,128)} %rows_in.1, s32[2,2,16]{2,1,0:T(2,128)} %cols_in.1, s32[2,2,16]{2,1,0:T(2,128)} %flags_in.1, ...), custom_call_target="tpu_custom_call" | custom-call | tf_op jit(solution)/shard_map/stefcal/pallas_call | solution.py:424
  35.3 1.5 %hand_on.1 = (f32[2,2,2,2048]{3,2,1,0:T(2,128)}, f32[4]{0:T(128)}) custom-call(f32[2,2,2,2048]{3,2,1,0:T(2,128)} %get-tuple-element.4.gains_in, f32[32,1,128]{2,1,0:T(1,128)} %get-tuple-element.5.stats_in), custom_call_target="tpu_custom_call" | custom-call | tf_op jit(solution)/shard_map/hand_on/pallas_call | solution.py:469
